TPU v7x, 256 devices: a whole 4x4x8 slice. The times are simulated.
256 devices in a mesh: gx: 8 (over z_hi, core), gy: 4 (over y), gz: 8 (over z_lo, x).
Axes of the slice: x: 4, y: 4, z: 8 (z_hi: 4, z_lo: 2; z = z_hi * 2 + z_lo), core: 2. Of those that a mesh axis runs over, the one named last changes fastest.
Arguments:
- field: float32 [256, 1024, 512], P('gz', 'gx', 'gy'), may hold values from -48 to 48
- factor_a: float32 [1024, 1024], replicated, may hold values from -0.5 to 3.5
- factor_b: float32 [512, 512], replicated, may hold values from -0.5 to 3.5
- factor_c: float32 [256, 256], replicated, may hold values from -0.5 to 3.5
Outputs:
- propagated: float32 [256, 1024, 512], P('gz', 'gx', 'gy')
All inputs are finite; a program needn't handle non-finite values.
Results may differ from a plain program's by a relative error of at most 0.00007.
Values sent between devices are 32-bit elements; how exact they have to be, the bound alone decides.
A program may use at most 64 MiB of HBM per device.

v0:
```python
import jax
import jax.numpy as jnp
from jax import lax
from jax.sharding import Mesh
from jax.sharding import PartitionSpec as P

GX = ("gx_0", "gx_1")
GX_GY = ("gx_0", "gx_1", "gy")
GZ = ("gz_0", "gz_1")
GX_GY_GZ = ("gx_0", "gx_1", "gy", "gz_0", "gz_1")


epsilon = 1e-06
target_ratio = 0.5


def split_up(value, dim, size):
    dims = value.shape
    tiles = value.reshape(*dims[:dim], size, dims[dim] // size, *dims[dim + 1 :])
    return jnp.moveaxis(tiles, dim, 0)


def laid_out(tiles, dim):
    dims = list(tiles.shape[1:])
    dims[dim] *= tiles.shape[0]
    return jnp.moveaxis(tiles, 0, dim).reshape(dims)


def joined_exchange(value, axis, axes, splits, concats):
    sizes = [lax.axis_size(a) for a in axes]
    tiles = split_up(value, splits[0], sizes[0])
    tiles = jnp.moveaxis(split_up(tiles, splits[1] + 1, sizes[1]), 0, 1)
    inside = tiles.shape[2:]
    tiles = tiles.reshape(-1, *inside)
    tiles = lax.all_to_all(tiles, axis, split_axis=0, concat_axis=0, tiled=True)
    tiles = laid_out(tiles.reshape(*sizes, *inside), concats[0] + 1)
    return laid_out(tiles, concats[1])


def over_axes(value, axes):
    for axis in axes:
        value = lax.psum(value, axis)
    return value


def on_device(field, factor_a, factor_b, factor_c):
    highest = lax.Precision.HIGHEST
    count_x = lax.axis_size(GX)
    count_y = lax.axis_size("gy")

    def slab_products(slabs):
        along_one = jnp.einsum("ip,mpj->mij", factor_a, slabs, precision=highest)
        along_two = jnp.einsum("mip,jp->mij", slabs, factor_b, precision=highest)
        return along_one + along_two

    def plane_terms(tensor):
        depth_home, width_one, width_two = tensor.shape
        depth = depth_home // (count_x * count_y)
        slabs = joined_exchange(tensor, GX_GY, (GX, "gy"), (0, 0), (1, 2))
        products = slab_products(slabs)
        returned = joined_exchange(products, GX_GY, (GX, "gy"), (1, 2), (0, 0))
        returned = returned.reshape(count_y, count_x, depth, width_one, width_two)
        return returned.transpose(1, 0, 2, 3, 4).reshape(depth_home, width_one, width_two)

    def fibre_product(fibres):
        flat = fibres.reshape(fibres.shape[0], -1)
        product = jnp.dot(factor_c, flat, precision=highest).reshape(fibres.shape)
        return lax.all_to_all(product, GZ, split_axis=0, concat_axis=1, tiled=True)

    def apply_block(tensor):
        planes = plane_terms(tensor)
        fibres = fibre_product(lax.all_to_all(tensor, GZ, split_axis=1, concat_axis=0, tiled=True))
        return planes + fibres

    first_term = apply_block(field)
    size_field, size_first = (
        over_axes(jnp.sum(field * field), GX_GY_GZ),
        over_axes(jnp.sum(first_term * first_term), GX_GY_GZ),
    )
    step = target_ratio * jnp.sqrt(size_field / (size_first + epsilon))
    second_term = apply_block(first_term)
    result = field - step * first_term + step * step / 2.0 * second_term
    return result


def solution(mesh):
    finer = Mesh(
        mesh.devices.reshape(4, 2, mesh.shape["gy"], 2, 4), ("gx_0", "gx_1", "gy", "gz_0", "gz_1")
    )
    in_specs = (P(GZ, GX, "gy"), P(), P(), P())
    out_specs = P(GZ, GX, "gy")
    return jax.shard_map(
        on_device, mesh=finer, in_specs=in_specs, out_specs=out_specs, check_vma=False
    )
```

profile of v0, /device:TPU:1, one launch (start us, length us, event | category | flops | bytes accessed | tf_op | source)
XLA Modules:
  0.0 403.5 jit_solution(6824693490417956613)
XLA Ops:
  0.0 2.9 copy.44
  2.9 31.8 %all_to_all.89 = f32[32,128,128]{2,0,1:T(8,128)} all-to-all(f32[32,128,128]{2,0,1:T(8,128)S(1)} %copy.44), channel_id=1, replica_groups=mesh['gx_0'=4,'gx_1'=2,'gy'=4,'gz_0'=2,'gz_1'=4] {'gz_0','gz_1'}, dimensions={1} | all-to-all | bytes 4194304 | tf_op jit(solution)/shard_map/all_to_all | solution.py:72
  34.7 12.8 %all-to-all-start = ((f32[32,1,128,128]{3,2,1,0:T(8,128)}), f32[32,1,128,128]{3,2,1,0:T(8,128)S(1)}, u32[]{:S(2)}, u32[]{:S(2)}) async-start(f32[32,1,128,128]{3,2,1,0:T(8,128)} %bitcast), calls=%async_computation | async-start | bytes 4194304 | tf_op jit(solution)/shard_map/all_to_all | solution.py:35
  52.5 3.0 copy.46
  55.5 3.5 fusion.7
  61.5 37.5 %all-to-all-done = f32[32,1,128,128]{3,2,1,0:T(8,128)S(1)} async-done(((f32[32,1,128,128]{3,2,1,0:T(8,128)}), f32[32,1,128,128]{3,2,1,0:T(8,128)S(1)}, u32[]{:S(2)}, u32[]{:S(2)}) %all-to-all-start) | async-done | bytes 2097184 | tf_op jit(solution)/shard_map/all_to_all | solution.py:35
  99.1 4.5 %all-to-all-start.3 = ((f32[256,16,128]{2,1,0:T(8,128)}), f32[256,16,128]{2,1,0:T(8,128)}, u32[]{:S(2)}, u32[]{:S(2)}) async-start(f32[256,16,128]{2,1,0:T(8,128)} %copy.47), calls=%async_computation.3 | async-start | bytes 4194304 | tf_op jit(solution)/shard_map/all_to_all | solution.py:68
  107.0 9.1 %fusion.9 = f32[512,1024]{1,0:T(8,128)S(1)} fusion(f32[1024,512]{0,1:T(8,128)S(1)} %bitcast.108, f32[1024,1024]{1,0:T(8,128)} %param.5), kind=kOutput, calls=%fused_computation.16 | convolution fusion | flops 6442450944 | bytes 8388608 | tf_op jit(solution)/shard_map/ip,mpj->mij/dot_general | solution.py:52
  116.1 3.5 fusion.4
  121.9 7.7 %all-to-all-done.3 = f32[256,16,128]{2,1,0:T(8,128)} async-done(((f32[256,16,128]{2,1,0:T(8,128)}), f32[256,16,128]{2,1,0:T(8,128)}, u32[]{:S(2)}, u32[]{:S(2)}) %all-to-all-start.3) | async-done | bytes 2097184 | tf_op jit(solution)/shard_map/all_to_all | solution.py:68
  129.6 5.5 %all-to-all-start.1 = ((f32[32,1,128,128]{3,2,1,0:T(8,128)}), f32[32,1,128,128]{3,2,1,0:T(8,128)S(1)}, u32[]{:S(2)}, u32[]{:S(2)}) async-start(f32[32,1,128,128]{3,2,1,0:T(8,128)} %bitcast.114), calls=%async_computation.1 | async-start | bytes 4194304 | tf_op jit(solution)/shard_map/all_to_all | solution.py:35
  135.2 3.2 copy.48
  138.4 37.1 %all-to-all-done.1 = f32[32,1,128,128]{3,2,1,0:T(8,128)S(1)} async-done(((f32[32,1,128,128]{3,2,1,0:T(8,128)}), f32[32,1,128,128]{3,2,1,0:T(8,128)S(1)}, u32[]{:S(2)}, u32[]{:S(2)}) %all-to-all-start.1) | async-done | bytes 2097184 | tf_op jit(solution)/shard_map/all_to_all | solution.py:35
  182.0 14.4 %all-to-all-start.6 = ((f32[32,128,128]{2,0,1:T(8,128)}), f32[32,128,128]{2,0,1:T(8,128)}, u32[]{:S(2)}, u32[]{:S(2)}) async-start(f32[32,128,128]{2,0,1:T(8,128)} %copy.53), calls=%async_computation.6 | async-start | bytes 4194304 | tf_op jit(solution)/shard_map/all_to_all | solution.py:72
  196.4 3.1 add.44
  199.6 23.1 %all-to-all-done.6 = f32[32,128,128]{2,0,1:T(8,128)} async-done(((f32[32,128,128]{2,0,1:T(8,128)}), f32[32,128,128]{2,0,1:T(8,128)}, u32[]{:S(2)}, u32[]{:S(2)}) %all-to-all-start.6) | async-done | bytes 2097184 | tf_op jit(solution)/shard_map/all_to_all | solution.py:72
  222.7 5.5 %all-to-all-start.4 = ((f32[32,1,128,128]{3,2,1,0:T(8,128)}), f32[32,1,128,128]{3,2,1,0:T(8,128)S(1)}, u32[]{:S(2)}, u32[]{:S(2)}) async-start(f32[32,1,128,128]{3,2,1,0:T(8,128)} %add.44), calls=%async_computation.4 | async-start | bytes 4194304 | tf_op jit(solution)/shard_map/all_to_all | solution.py:35
  231.0 5.0 %fusion = f32[2048,256]{1,0:T(8,128)} fusion(f32[256,256]{1,0:T(8,128)S(1)} %copy-done.3, f32[32,8,16,128]{3,2,1,0:T(8,128)S(1)} %bitcast.121), kind=kOutput, calls=%fused_computation | convolution fusion | flops 1610612736 | bytes 4456448 | tf_op jit(solution)/shard_map/dot_general | solution.py:67
  236.0 3.1 copy.55
  239.1 29.2 %all-to-all-done.4 = f32[32,1,128,128]{3,2,1,0:T(8,128)S(1)} async-done(((f32[32,1,128,128]{3,2,1,0:T(8,128)}), f32[32,1,128,128]{3,2,1,0:T(8,128)S(1)}, u32[]{:S(2)}, u32[]{:S(2)}) %all-to-all-start.4) | async-done | bytes 2097184 | tf_op jit(solution)/shard_map/all_to_all | solution.py:35
  268.3 14.6 %all-to-all-start.7 = ((f32[256,16,128]{2,1,0:T(8,128)}), f32[256,16,128]{2,1,0:T(8,128)}, u32[]{:S(2)}, u32[]{:S(2)}) async-start(f32[256,16,128]{2,1,0:T(8,128)} %copy.55), calls=%async_computation.7 | async-start | bytes 4194304 | tf_op jit(solution)/shard_map/all_to_all | solution.py:68
  286.3 9.1 %fusion.10 = f32[512,1024]{1,0:T(8,128)S(1)} fusion(f32[1024,512]{0,1:T(8,128)S(1)} %bitcast.110, f32[1024,1024]{1,0:T(8,128)} %param.5), kind=kOutput, calls=%fused_computation.17 | convolution fusion | flops 6442450944 | bytes 8388608 | tf_op jit(solution)/shard_map/ip,mpj->mij/dot_general | solution.py:52
  295.4 3.5 fusion.3
  301.2 8.0 %all-to-all-done.7 = f32[256,16,128]{2,1,0:T(8,128)} async-done(((f32[256,16,128]{2,1,0:T(8,128)}), f32[256,16,128]{2,1,0:T(8,128)}, u32[]{:S(2)}, u32[]{:S(2)}) %all-to-all-start.7) | async-done | bytes 2097184 | tf_op jit(solution)/shard_map/all_to_all | solution.py:68
  309.2 5.5 %all-to-all-start.5 = ((f32[32,1,128,128]{3,2,1,0:T(8,128)}), f32[32,1,128,128]{3,2,1,0:T(8,128)}, u32[]{:S(2)}, u32[]{:S(2)}) async-start(f32[32,1,128,128]{3,2,1,0:T(8,128)} %bitcast.30), calls=%async_computation.5 | async-start | bytes 4194304 | tf_op jit(solution)/shard_map/all_to_all | solution.py:35
  317.4 39.7 %all-reduce.2 = (f32[]{:T(128)}, f32[]{:T(128)}) all-reduce(f32[]{:T(128)} %multiply_reduce_fusion.1, f32[]{:T(128)} %get-tuple-element.15), channel_id=1, replica_groups=mesh['gx_0'=4,'gx_1'=2,'gy'=4,'gz_0'=2,'gz_1'=4] {'gx_0'}, use_global_device_ids=true, to_apply=%region_1.0 | all-reduce | flops 2 | bytes 16 | tf_op jit(solution)/shard_map/psum | solution.py:42
  357.1 9.8 %all-reduce.4 = (f32[]{:T(128)}, f32[]{:T(128)}) all-reduce(f32[]{:T(128)} %get-tuple-element.9, f32[]{:T(128)} %get-tuple-element.10), channel_id=1, replica_groups=mesh['gx_0'=4,'gx_1'=2,'gy'=4,'gz_0'=2,'gz_1'=4] {'gx_1'}, use_global_device_ids=true, to_apply=%region_2.0 | all-reduce | flops 2 | bytes 16 | tf_op jit(solution)/shard_map/psum | solution.py:42
  366.9 9.6 %all-reduce.1 = (f32[]{:T(128)}, f32[]{:T(128)}) all-reduce(f32[]{:T(128)} %get-tuple-element.13, f32[]{:T(128)} %get-tuple-element.14), channel_id=1, replica_groups=mesh['gx_0'=4,'gx_1'=2,'gy'=4,'gz_0'=2,'gz_1'=4] {'gy'}, use_global_device_ids=true, to_apply=%region_3.0 | all-reduce | flops 2 | bytes 16 | tf_op jit(solution)/shard_map/psum | solution.py:42
  376.5 9.5 %all-reduce.3 = (f32[]{:T(128)}, f32[]{:T(128)}) all-reduce(f32[]{:T(128)} %get-tuple-element.7, f32[]{:T(128)} %get-tuple-element.8), channel_id=1, replica_groups=mesh['gx_0'=4,'gx_1'=2,'gy'=4,'gz_0'=2,'gz_1'=4] {'gz_0'}, use_global_device_ids=true, to_apply=%region_4.0 | all-reduce | flops 2 | bytes 16 | tf_op jit(solution)/shard_map/psum | solution.py:42
  386.0 7.7 %all-reduce = (f32[]{:T(128)}, f32[]{:T(128)}) all-reduce(f32[]{:T(128)} %get-tuple-element.11, f32[]{:T(128)} %get-tuple-element.12), channel_id=1, replica_groups=mesh['gx_0'=4,'gx_1'=2,'gy'=4,'gz_0'=2,'gz_1'=4] {'gz_1'}, use_global_device_ids=true, to_apply=%region_5.0 | all-reduce | flops 2 | bytes 16 | tf_op jit(solution)/shard_map/psum | solution.py:42
  395.1 3.4 copy.56
  398.4 5.1 %fusion.6 = f32[32,128,128]{2,1,0:T(8,128)} fusion(f32[32,8,16,128]{3,2,1,0:T(8,128)} %copy.56, f32[32,1,128,128]{3,2,1,0:T(8,128)} %all-to-all-done.5, f32[32,128,128]{2,1,0:T(8,128)} %param.4, f32[32,128,128]{2,1,0:T(8,128)S(1)} %copy-done.2, f32[]{:T(128)S(6)} %div.7, f32[]{:T(128)S(6)} %mul_shard_map.3), kind=kLoop, calls=%fused_computation.11 | loop fusion | flops 2621440 | bytes 10485768 | tf_op jit(solution)/shard_map/add | solution.py:82
  (24 shorter events, 31.0 us)
Async XLA Ops:
  0.0 116.1 %copy-start = (f32[512,512]{1,0:T(8,128)S(1)}, f32[512,512]{1,0:T(8,128)}, u32[]{:S(2)}) copy-start(f32[512,512]{1,0:T(8,128)} %param.6) | copy-start | bytes 3145732
  34.7 64.3 %all-to-all-start = ((f32[32,1,128,128]{3,2,1,0:T(8,128)}), f32[32,1,128,128]{3,2,1,0:T(8,128)S(1)}, u32[]{:S(2)}, u32[]{:S(2)}) async-start(f32[32,1,128,128]{3,2,1,0:T(8,128)} %bitcast), calls=%async_computation | async-start | bytes 4194304 | tf_op jit(solution)/shard_map/all_to_all | solution.py:35
  52.5 3.0 copy-start.3
  99.1 30.5 %all-to-all-start.3 = ((f32[256,16,128]{2,1,0:T(8,128)}), f32[256,16,128]{2,1,0:T(8,128)}, u32[]{:S(2)}, u32[]{:S(2)}) async-start(f32[256,16,128]{2,1,0:T(8,128)} %copy.47), calls=%async_computation.3 | async-start | bytes 4194304 | tf_op jit(solution)/shard_map/all_to_all | solution.py:68
  129.6 45.8 %all-to-all-start.1 = ((f32[32,1,128,128]{3,2,1,0:T(8,128)}), f32[32,1,128,128]{3,2,1,0:T(8,128)S(1)}, u32[]{:S(2)}, u32[]{:S(2)}) async-start(f32[32,1,128,128]{3,2,1,0:T(8,128)} %bitcast.114), calls=%async_computation.1 | async-start | bytes 4194304 | tf_op jit(solution)/shard_map/all_to_all | solution.py:35
  178.1 1.3 copy-start.1
  182.0 40.7 %all-to-all-start.6 = ((f32[32,128,128]{2,0,1:T(8,128)}), f32[32,128,128]{2,0,1:T(8,128)}, u32[]{:S(2)}, u32[]{:S(2)}) async-start(f32[32,128,128]{2,0,1:T(8,128)} %copy.53), calls=%async_computation.6 | async-start | bytes 4194304 | tf_op jit(solution)/shard_map/all_to_all | solution.py:72
  222.7 45.6 %all-to-all-start.4 = ((f32[32,1,128,128]{3,2,1,0:T(8,128)}), f32[32,1,128,128]{3,2,1,0:T(8,128)S(1)}, u32[]{:S(2)}, u32[]{:S(2)}) async-start(f32[32,1,128,128]{3,2,1,0:T(8,128)} %add.44), calls=%async_computation.4 | async-start | bytes 4194304 | tf_op jit(solution)/shard_map/all_to_all | solution.py:35
  268.3 40.9 %all-to-all-start.7 = ((f32[256,16,128]{2,1,0:T(8,128)}), f32[256,16,128]{2,1,0:T(8,128)}, u32[]{:S(2)}, u32[]{:S(2)}) async-start(f32[256,16,128]{2,1,0:T(8,128)} %copy.55), calls=%async_computation.7 | async-start | bytes 4194304 | tf_op jit(solution)/shard_map/all_to_all | solution.py:68
  309.2 89.2 %all-to-all-start.5 = ((f32[32,1,128,128]{3,2,1,0:T(8,128)}), f32[32,1,128,128]{3,2,1,0:T(8,128)}, u32[]{:S(2)}, u32[]{:S(2)}) async-start(f32[32,1,128,128]{3,2,1,0:T(8,128)} %bitcast.30), calls=%async_computation.5 | async-start | bytes 4194304 | tf_op jit(solution)/shard_map/all_to_all | solution.py:35
  395.1 3.4 copy-start.2
where the time goes:
time: 408 us; the launch traced here: 403 us
  waiting for transfers between devices  143 us (35%)
  blocking collectives  108 us (26%)
  starting transfers between devices  62.8 us (15%)
  local copies, waits for them, and re-layouts  41 us (10%)
  matrix products  33.8 us (8%)
  other arithmetic  13.7 us (3%)
    all_to_all x4, waiting for transfers between devices, joined_exchange(): tiles = lax.all_to_all(tiles, axis, split_axis=0, concat_axis=0, tiled=True)  104 us
    psum x5, blocking collectives, over_axes(): value = lax.psum(value, axis)  76.3 us
    all_to_all x1, blocking collectives, apply_block(): lax.all_to_all(tensor, GZ, split_axis=1, concat_axis=0, tiled=True)  31.8 us
    all_to_all x4, starting transfers between devices, joined_exchange(): tiles = lax.all_to_all(tiles, axis, split_axis=0, concat_axis=0, tiled=True)  29.2 us
    all_to_all x1, waiting for transfers between devices, apply_block(): lax.all_to_all(tensor, GZ, split_axis=1, concat_axis=0, tiled=True)  23.1 us
    all_to_all x2, starting transfers between devices, fibre_product(): return lax.all_to_all(product, GZ, split_axis=0, concat_axis=1, tiled=True)  19.2 us
    dot_general x2, matrix products, slab_products(): along_one = jnp.einsum('ip,mpj->mij', factor_a, slabs, precision=highest)  18.1 us
    all_to_all x2, waiting for transfers between devices, fibre_product(): return lax.all_to_all(product, GZ, split_axis=0, concat_axis=1, tiled=True)  15.7 us
  transfers between devices with their start and end apart: 7, of which 6 were waited for; matrix products, arithmetic and copies ran while one was open for 18% of the time, Pallas kernels for 0%

commit v1 on v0

v1 whole, which is shorter than its diff:
```python
import functools

import jax
import jax.numpy as jnp
from jax import lax
from jax.experimental import pallas as pl
from jax.experimental.pallas import tpu as pltpu
from jax.sharding import PartitionSpec as P

MESH = pl.DeviceIdType.MESH
F32, BF16 = jnp.float32, jnp.bfloat16

epsilon = 1e-06
target_ratio = 0.5

GX, GY, GZ = 8, 4, 8
GROUP = GX * GZ
BK, BI, BJ = 32, 128, 128
N1, N2, N3 = 1024, 512, 256
KY = BK // GY
PHASES = 2


def split(x):
    hi = x.astype(BF16)
    return hi, (x - hi.astype(F32)).astype(BF16)


def dot(a, b):
    return jnp.dot(a, b, preferred_element_type=F32)


def dot_t(a, b):
    return lax.dot_general(a, b, (((1,), (1,)), ((), ())), preferred_element_type=F32)


def member(t, gx, gz):
    z, x, c = (gx // 2) * 2 + gz // 4, gz % 4, gx % 2
    m, rest = t // 8, t % 8
    odd = m % 2
    dz = odd * ((m + 1) // 2) + (1 - odd) * (8 - m // 2)
    z2 = (z + dz) % 8
    x2 = (x + rest // 2) % 4
    c2 = (c + rest) % 2
    return (z2 // 2) * 2 + c2, (z2 % 2) * 4 + x2


def kernel(
    ft, a_hbm, b_hbm, c_hbm, out,
    a_f, b_f, c_f, a_h, a_l, b_h, b_l, c_h, c_l,
    wide, s_one, s_two, x_h, x_l,
    one_home, two_home, b_home, w_home,
    line_f, line_b, line_s, line_w,
    norm_src, norm_y, norm_mid, norm_all,
    load_sem, zs_sem, zr_sem, ys_sem, yr_sem, ns_sem, nr_sem,
):
    gx, gy, gz = lax.axis_index("gx"), lax.axis_index("gy"), lax.axis_index("gz")
    mine = gx * GZ + gz

    loads = [
        pltpu.make_async_copy(src, dst, load_sem.at[n])
        for n, (src, dst) in enumerate(((c_hbm, c_f), (a_hbm, a_f), (b_hbm, b_f)))
    ]
    for copy in loads:
        copy.start()

    barrier = pltpu.get_barrier_semaphore()

    def greet(t, carry):
        px, pz = member(t, gx, gz)
        pl.semaphore_signal(barrier, inc=1, device_id={"gx": px, "gz": pz}, device_id_type=MESH)
        return carry

    lax.fori_loop(1, GROUP, greet, 0)
    for d in range(1, GY):
        pl.semaphore_signal(
            barrier, inc=1, device_id={"gy": (gy + d) % GY}, device_id_type=MESH
        )
    pl.semaphore_wait(barrier, GROUP - 1 + GY - 1)

    def to_wide(p):
        def send(t, carry):
            px, pz = member(t, gx, gz)
            pltpu.make_async_remote_copy(
                src_ref=ft.at[p * GROUP + px * GZ + pz],
                dst_ref=wide.at[p, pl.ds(gz * BK, BK), pl.ds(gx * BI, BI)],
                send_sem=zs_sem.at[p], recv_sem=zr_sem.at[p],
                device_id={"gx": px, "gz": pz}, device_id_type=MESH,
            ).start()
            return carry

        lax.fori_loop(1, GROUP, send, 0)
        pltpu.make_async_copy(
            ft.at[p * GROUP + mine],
            wide.at[p, pl.ds(gz * BK, BK), pl.ds(gx * BI, BI)],
            zr_sem.at[p],
        ).start()

    def to_home(n, src, dst, p):
        slot = PHASES * n + p

        def send(t, carry):
            px, pz = member(t, gx, gz)
            pltpu.make_async_remote_copy(
                src_ref=src.at[p, pl.ds(pz * BK, BK), pl.ds(px * BI, BI)],
                dst_ref=dst.at[p * GROUP + mine],
                send_sem=zs_sem.at[slot], recv_sem=zr_sem.at[slot],
                device_id={"gx": px, "gz": pz}, device_id_type=MESH,
            ).start()
            return carry

        lax.fori_loop(1, GROUP, send, 0)
        pltpu.make_async_copy(
            src.at[p, pl.ds(gz * BK, BK), pl.ds(gx * BI, BI)],
            dst.at[p * GROUP + mine],
            zr_sem.at[slot],
        ).start()

    def wait_z(slot, ref):
        pltpu.make_async_copy(ref, ref, zr_sem.at[slot]).wait()

    def to_line(slot, src, dst, j0, rows):
        for d in range(1, GY):
            py = (gy + d) % GY
            pltpu.make_async_remote_copy(
                src_ref=src.at[pl.ds(j0, rows), pl.ds(py * KY, KY), :],
                dst_ref=dst.at[pl.ds(gy * BJ + j0, rows)],
                send_sem=ys_sem.at[slot], recv_sem=yr_sem.at[slot],
                device_id={"gy": py}, device_id_type=MESH,
            ).start()
        pltpu.make_async_copy(
            src.at[pl.ds(j0, rows), pl.ds(gy * KY, KY), :],
            dst.at[pl.ds(gy * BJ + j0, rows)],
            yr_sem.at[slot],
        ).start()

    def from_line(slot, src, dst):
        for d in range(1, GY):
            py = (gy + d) % GY
            pltpu.make_async_remote_copy(
                src_ref=src.at[pl.ds(py * BJ, BJ)],
                dst_ref=dst.at[:, pl.ds(gy * KY, KY), :],
                send_sem=ys_sem.at[slot], recv_sem=yr_sem.at[slot],
                device_id={"gy": py}, device_id_type=MESH,
            ).start()
        pltpu.make_async_copy(
            src.at[pl.ds(gy * BJ, BJ)],
            dst.at[:, pl.ds(gy * KY, KY), :],
            yr_sem.at[slot],
        ).start()

    def wait_y(slot, ref):
        pltpu.make_async_copy(ref, ref, yr_sem.at[slot]).wait()

    to_wide(0)
    to_line(0, ft, line_f, 0, BJ)
    to_wide(1)

    for copy in loads:
        copy.wait()
    c_h[...], c_l[...] = split(c_f[...])
    b_h[...], b_l[...] = split(b_f[...])

    def split_a(n, carry):
        rows = pl.ds(pl.multiple_of(n * 128, 128), 128)
        a_h[rows, :], a_l[rows, :] = split(a_f[rows, :])
        return carry

    lax.fori_loop(0, N1 // 128, split_a, 0)

    def along_wide(src, dst, p):
        def cut(n, carry):
            rows = pl.ds(pl.multiple_of(n * 64, 64), 64)
            x_h[rows, :], x_l[rows, :] = split(src[p, rows, :])
            return carry

        lax.fori_loop(0, N3 // 64, cut, 0)

        def tile(n, carry):
            cols = pl.ds(pl.multiple_of(n * 256, 256), 256)
            a_hi, a_lo = a_h[cols, :], a_l[cols, :]
            total = dot_t(x_h[...], a_hi) + dot_t(x_l[...], a_hi) + dot_t(x_h[...], a_lo)
            xh, xl = x_h[:, cols], x_l[:, cols]
            total = total + dot(c_h[...], xh) + dot(c_l[...], xh) + dot(c_h[...], xl)
            dst[p, :, cols] = total
            return carry

        lax.fori_loop(0, N1 // 256, tile, 0)

    def along_line(src, put):
        flat = src.reshape(N2 * KY, BI)

        def pair(q, carry):
            cols = [flat[pl.ds(2 * q + e, N2, stride=KY), :] for e in range(2)]
            xh, xl = split(jnp.concatenate(cols, axis=1))
            total = dot(b_h[...], xh) + dot(b_l[...], xh) + dot(b_h[...], xl)
            for e in range(2):
                put(pl.ds(2 * q + e, N2, stride=KY), total[:, e * BI:(e + 1) * BI])
            return carry

        lax.fori_loop(0, KY // 2, pair, 0)

    flat_b, flat_w = line_b.reshape(N2 * KY, BI), line_w.reshape(N2 * KY, BI)

    def put_b(rows, value):
        flat_b[rows, :] = value

    def put_w(rows, value):
        flat_w[rows, :] = value

    def add_w(rows, value):
        flat_w[rows, :] = flat_w[rows, :] + 2.0 * value

    wait_z(0, wide.at[0])
    along_wide(wide, s_one, 0)
    to_home(1, s_one, one_home, 0)

    wait_y(0, line_f)
    along_line(line_f, put_b)
    from_line(1, line_b, b_home)
    along_wide(s_one, s_two, 0)
    along_line(line_b, put_w)

    wait_z(1, wide.at[1])
    along_wide(wide, s_one, 1)
    to_home(1, s_one, one_home, 1)
    to_home(2, s_two, two_home, 0)
    along_wide(s_one, s_two, 1)

    def squares(read):
        def add(n, carry):
            v = read(pl.ds(n * 8, 8))
            return carry + jnp.sum(v * v, axis=(0, 1)).reshape(1, BI)

        return add

    zero = jnp.zeros((1, BI), F32)
    of_field = lax.fori_loop(0, BJ // 8, squares(lambda r: ft[r]), zero)
    wait_y(1, b_home)

    wait_z(2, one_home.at[pl.ds(0, GROUP)])
    to_line(2, one_home, line_s, 0, GROUP)
    first = squares(lambda r: one_home[r] + b_home[r])
    of_first = lax.fori_loop(0, GROUP // 8, first, zero)
    wait_z(3, one_home.at[pl.ds(GROUP, GROUP)])
    to_line(3, one_home, line_s, GROUP, GROUP)
    of_first = lax.fori_loop(GROUP // 8, BJ // 8, first, of_first)

    lane = lax.broadcasted_iota(jnp.int32, (1, BI), 1)
    norm_src[0] = jnp.where(lane == 0, jnp.sum(of_field), jnp.sum(of_first))

    def send_norm_y():
        for d in range(1, GY):
            pltpu.make_async_remote_copy(
                src_ref=norm_src, dst_ref=norm_y.at[pl.ds(gy, 1)],
                send_sem=ns_sem.at[0], recv_sem=nr_sem.at[0],
                device_id={"gy": (gy + d) % GY}, device_id_type=MESH,
            ).start()
        pltpu.make_async_copy(norm_src, norm_y.at[pl.ds(gy, 1)], nr_sem.at[0]).start()

    send_norm_y()
    to_home(2, s_two, two_home, 1)
    pltpu.make_async_copy(norm_y, norm_y, nr_sem.at[0]).wait()
    norm_mid[0] = norm_y[0] + norm_y[1] + norm_y[2] + norm_y[3]

    def send_norm(t, carry):
        px, pz = member(t, gx, gz)
        pltpu.make_async_remote_copy(
            src_ref=norm_mid, dst_ref=norm_all.at[pl.ds(mine, 1)],
            send_sem=ns_sem.at[1], recv_sem=nr_sem.at[1],
            device_id={"gx": px, "gz": pz}, device_id_type=MESH,
        ).start()
        return carry

    lax.fori_loop(1, GROUP, send_norm, 0)
    pltpu.make_async_copy(norm_mid, norm_all.at[pl.ds(mine, 1)], nr_sem.at[1]).start()

    wait_y(2, line_s.at[pl.ds(0, N2 // 2)])
    wait_y(3, line_s.at[pl.ds(0, N2 // 2)])
    along_line(line_s, add_w)
    from_line(4, line_w, w_home)

    pltpu.make_async_copy(norm_all, norm_all, nr_sem.at[1]).wait()
    sums = jnp.sum(norm_all[...], axis=0)
    size_field = jnp.sum(jnp.where(lane == 0, sums, 0.0))
    size_first = jnp.sum(jnp.where(lane == 1, sums, 0.0))
    ratio = jnp.full((1, BI), size_field, F32) / (jnp.full((1, BI), size_first, F32) + epsilon)
    step = (target_ratio * jnp.sqrt(ratio)).reshape(1, 1, BI)
    half = step * step / 2.0

    wait_z(4, two_home.at[pl.ds(0, GROUP)])
    wait_y(4, w_home)

    def finish(n, carry):
        r = pl.ds(n * 4, 4)
        out[r] = (ft[r] - step * (one_home[r] + b_home[r])) + half * (two_home[r] + w_home[r])
        return carry

    lax.fori_loop(0, GROUP // 4, finish, 0)
    wait_z(5, two_home.at[pl.ds(GROUP, GROUP)])
    lax.fori_loop(GROUP // 4, BJ // 4, finish, 0)

    for slot in range(6):
        sent = ft.at[pl.ds(0, GROUP - 1)]
        pltpu.make_async_copy(sent, sent, zs_sem.at[slot]).wait()
    for slot, rows in ((0, 3 * BJ), (1, 3 * BJ), (2, 3 * GROUP), (3, 3 * GROUP), (4, 3 * BJ)):
        sent = line_f.at[pl.ds(0, rows)]
        pltpu.make_async_copy(sent, sent, ys_sem.at[slot]).wait()
    sent = norm_y.at[pl.ds(0, GY - 1)]
    pltpu.make_async_copy(sent, sent, ns_sem.at[0]).wait()
    sent = norm_all.at[pl.ds(0, GROUP - 1)]
    pltpu.make_async_copy(sent, sent, ns_sem.at[1]).wait()


def on_device(field, factor_a, factor_b, factor_c):
    turned = jnp.transpose(field, (2, 0, 1))
    home = (BJ, BK, BI)
    vmem = pltpu.VMEM
    dma = pltpu.SemaphoreType.DMA
    scratch = [
        vmem((N1, N1), F32), vmem((N2, N2), F32), vmem((N3, N3), F32),
        vmem((N1, N1), BF16), vmem((N1, N1), BF16),
        vmem((N2, N2), BF16), vmem((N2, N2), BF16),
        vmem((N3, N3), BF16), vmem((N3, N3), BF16),
        vmem((PHASES, N3, N1), F32), vmem((PHASES, N3, N1), F32), vmem((PHASES, N3, N1), F32),
        vmem((N3, N1), BF16), vmem((N3, N1), BF16),
        vmem(home, F32), vmem(home, F32), vmem(home, F32), vmem(home, F32),
        vmem((N2, KY, BI), F32), vmem((N2, KY, BI), F32),
        vmem((N2, KY, BI), F32), vmem((N2, KY, BI), F32),
        vmem((1, 1, BI), F32), vmem((GY, 1, BI), F32),
        vmem((1, 1, BI), F32), vmem((GROUP, 1, BI), F32),
        dma((3,)), dma((6,)), dma((6,)), dma((5,)), dma((5,)), dma((2,)), dma((2,)),
    ]
    result = pl.pallas_call(
        kernel,
        out_shape=jax.ShapeDtypeStruct(home, F32),
        in_specs=[pl.BlockSpec(memory_space=pltpu.VMEM)] + [pl.BlockSpec(memory_space=pl.ANY)] * 3,
        out_specs=pl.BlockSpec(memory_space=pltpu.VMEM),
        scratch_shapes=scratch,
        compiler_params=pltpu.CompilerParams(
            collective_id=0, has_side_effects=True, vmem_limit_bytes=60 * 1024 * 1024
        ),
        name="taylor",
    )(turned, factor_a, factor_b, factor_c)
    return jnp.transpose(result, (1, 2, 0))


def solution(mesh):
    return jax.shard_map(
        on_device, mesh=mesh, in_specs=(P("gz", "gx", "gy"), P(), P(), P()),
        out_specs=P("gz", "gx", "gy"), check_vma=False,
    )
```

time: 408 us -> 162 us (0.40); the launches traced: 403 us -> 162 us
  Pallas kernels: 0 us -> 156 us
  waiting for transfers between devices: 143 us -> 0 us
  blocking collectives: 108 us -> 0 us
  starting transfers between devices: 62.8 us -> 0 us
  local copies, waits for them, and re-layouts: 41 us -> 6 us
  matrix products: 33.8 us -> 0 us
  other arithmetic: 13.7 us -> 0 us
    pallas_call x0 -> x1, Pallas kernels: none -> 156 us  [on_device(): pl.pallas_call(kernel, out_shape=jax.ShapeDtypeStruct(home, F32), in_spec...]
    all_to_all x7 -> x0, waiting for transfers between devices: 143 us -> none  [the longest x4 104 us: joined_exchange(): tiles = lax.all_to_all(tiles, axis, split_axis=0, concat_axis=0, tiled=True)]
    psum x5 -> x0, blocking collectives: 76.3 us -> none  [over_axes(): value = lax.psum(value, axis)]
    all_to_all x7 -> x0, starting transfers between devices: 62.8 us -> none  [the longest x4 29.2 us: joined_exchange(): tiles = lax.all_to_all(tiles, axis, split_axis=0, concat_axis=0, tiled=True)]
    dot_general x6 -> x0, matrix products: 33.8 us -> none  [the longest x2 18.1 us: slab_products(): along_one = jnp.einsum('ip,mpj->mij', factor_a, slabs, precision=highest)]
    all_to_all x1 -> x0, blocking collectives: 31.8 us -> none  [apply_block(): lax.all_to_all(tensor, GZ, split_axis=1, concat_axis=0, tiled=True)]
    all_to_all x4 -> x0, local copies, waits for them, and re-layouts: 12.1 us -> none  [the longest x2 6.55 us: fibre_product(): return lax.all_to_all(product, GZ, split_axis=0, concat_axis=1, tiled=True)]
    add x2 -> x0, other arithmetic: 8.2 us -> none  [the longest x1 5.05 us: on_device(): result = field - step * first_term + step * step / 2.0 * second_term]
  transfers between devices with their start and end apart: 7 -> 0, of which waited for: 6 -> 0; matrix products, arithmetic and copies ran while one was open for 18% -> 0% of each run, Pallas kernels for 0% -> 0%
where the time goes in v1:
time: 162 us
  Pallas kernels  156 us (96%)
  local copies, waits for them, and re-layouts  6 us (4%)
    pallas_call x1, Pallas kernels, on_device(): pl.pallas_call(kernel, out_shape=jax.ShapeDtypeStruct(home, F32), in_spec...  156 us

profile of v1, /device:TPU:1, one launch (start us, length us, event | category | flops | bytes accessed | tf_op | source)
XLA Modules:
  0.0 161.9 jit_solution(5351198271506588101)
XLA Ops:
  0.0 3.0 %copy.5 = f32[32,128,128]{1,0,2:T(8,128)} copy(f32[32,128,128]{2,1,0:T(8,128)} %param.4) | data formatting | bytes 4194304 | tf_op args[0]
  3.0 155.9 %taylor.1 = f32[128,32,128]{2,1,0:T(8,128)} custom-call(f32[128,32,128]{2,1,0:T(8,128)} %bitcast.3, f32[1024,1024]{1,0:T(8,128)} %a_hbm.1, f32[512,512]{1,0:T(8,128)} %b_hbm.1, f32[256,256]{1,0:T(8,128)} %c_hbm.1), custom_call_target="tpu_custom_call" | custom-call | tf_op jit(solution)/shard_map/taylor/pallas_call | solution.py:334
  158.9 3.0 %copy.6 = f32[32,128,128]{2,1,0:T(8,128)} copy(f32[32,128,128]{1,0,2:T(8,128)} %bitcast.2) | data formatting | bytes 4194304 | tf_op jit(solution)/shard_map/transpose | solution.py:345

commit v2 on v1

--- a/solution.py
+++ b/solution.py
@@ -19,6 +19,8 @@
 N1, N2, N3 = 1024, 512, 256
 KY = BK // GY
 PHASES = 2
+SIDES = 2
+HALF = GROUP // SIDES
 
 
 def split(x):
@@ -45,9 +47,14 @@
     return (z2 // 2) * 2 + c2, (z2 % 2) * 4 + x2
 
 
+def device_at(z, x, c):
+    z, x, c = z % 8, x % 4, c % 2
+    return (z // 2) * 2 + c, (z % 2) * 4 + x
+
+
 def kernel(
-    ft, a_hbm, b_hbm, c_hbm, out,
-    a_f, b_f, c_f, a_h, a_l, b_h, b_l, c_h, c_l,
+    field, a_hbm, b_hbm, c_hbm, out,
+    ft, b_f, c_f, a_h, a_l, b_h, b_l, c_h, c_l,
     wide, s_one, s_two, x_h, x_l,
     one_home, two_home, b_home, w_home,
     line_f, line_b, line_s, line_w,
@@ -56,10 +63,12 @@
 ):
     gx, gy, gz = lax.axis_index("gx"), lax.axis_index("gy"), lax.axis_index("gz")
     mine = gx * GZ + gz
-
+    z, x, c = (gx // 2) * 2 + gz // 4, gz % 4, gx % 2
+
+    pieces = [(c_hbm, c_f), (b_hbm, b_f)]
+    pieces += [(a_hbm.at[pl.ds(n * N3, N3)], s_two.at[n]) for n in range(N1 // N3)]
     loads = [
-        pltpu.make_async_copy(src, dst, load_sem.at[n])
-        for n, (src, dst) in enumerate(((c_hbm, c_f), (a_hbm, a_f), (b_hbm, b_f)))
+        pltpu.make_async_copy(src, dst, load_sem.at[n]) for n, (src, dst) in enumerate(pieces)
     ]
     for copy in loads:
         copy.start()
@@ -76,48 +85,81 @@
         pl.semaphore_signal(
             barrier, inc=1, device_id={"gy": (gy + d) % GY}, device_id_type=MESH
         )
+
+    flat_ft = ft.reshape(BJ * BK, BI)
+
+    def turn(k, carry):
+        flat_ft[pl.ds(k, BJ, stride=BK), :] = field[k].T
+        return carry
+
+    lax.fori_loop(0, BK, turn, 0)
     pl.semaphore_wait(barrier, GROUP - 1 + GY - 1)
 
-    def to_wide(p):
-        def send(t, carry):
-            px, pz = member(t, gx, gz)
-            pltpu.make_async_remote_copy(
-                src_ref=ft.at[p * GROUP + px * GZ + pz],
-                dst_ref=wide.at[p, pl.ds(gz * BK, BK), pl.ds(gx * BI, BI)],
-                send_sem=zs_sem.at[p], recv_sem=zr_sem.at[p],
+    def to_near(p, side):
+        sign = 1 - 2 * side
+
+        def place(u):
+            up = sign * (u // 8)
+            px, pz = device_at(z + up, x + u // 2, c + u)
+            ox, oz = device_at(z + up - side, x + u // 2, c + u)
+            src = ft.at[p * GROUP + ox * GZ + oz]
+            dst = wide.at[2 * p + side, pl.ds(gz * BK, BK), pl.ds(gx * BI, BI)]
+            return px, pz, src, dst
+
+        def send(u, carry):
+            px, pz, src, dst = place(u)
+            pltpu.make_async_remote_copy(
+                src_ref=src, dst_ref=dst,
+                send_sem=zs_sem.at[2 * p + side], recv_sem=zr_sem.at[2 * p + side],
                 device_id={"gx": px, "gz": pz}, device_id_type=MESH,
             ).start()
             return carry
 
-        lax.fori_loop(1, GROUP, send, 0)
-        pltpu.make_async_copy(
-            ft.at[p * GROUP + mine],
-            wide.at[p, pl.ds(gz * BK, BK), pl.ds(gx * BI, BI)],
-            zr_sem.at[p],
-        ).start()
-
-    def to_home(n, src, dst, p):
-        slot = PHASES * n + p
-
-        def send(t, carry):
-            px, pz = member(t, gx, gz)
-            pltpu.make_async_remote_copy(
-                src_ref=src.at[p, pl.ds(pz * BK, BK), pl.ds(px * BI, BI)],
-                dst_ref=dst.at[p * GROUP + mine],
-                send_sem=zs_sem.at[slot], recv_sem=zr_sem.at[slot],
+        lax.fori_loop(1, HALF, send, 0)
+        _, _, src, dst = place(0)
+        pltpu.make_async_copy(src, dst, zr_sem.at[2 * p + side]).start()
+
+    def swap(p, side):
+        sign = 1 - 2 * side
+        px, pz = device_at(z + sign, x, c)
+        for n in range(4):
+            from_z = (z - sign * n) % 8
+            rows = pl.ds((from_z % 2) * (N3 // 2), N3 // 2)
+            cols = pl.ds((from_z // 2) * (N1 // 4), N1 // 4)
+            pltpu.make_async_remote_copy(
+                src_ref=wide.at[2 * p + side, rows, cols],
+                dst_ref=wide.at[2 * p + 1 - side, rows, cols],
+                send_sem=zs_sem.at[4 + 2 * p + side], recv_sem=zr_sem.at[4 + 2 * p + 1 - side],
                 device_id={"gx": px, "gz": pz}, device_id_type=MESH,
             ).start()
+
+    def to_home(n, src, dst, p, side):
+        sign = 1 - 2 * side
+        ox, oz = device_at(z - side, x, c)
+        row = p * GROUP + ox * GZ + oz
+
+        def place(u):
+            px, pz = device_at(z - sign * (u // 8), x + u // 2, c + u)
+            return px, pz, src.at[2 * p + side, pl.ds(pz * BK, BK), pl.ds(px * BI, BI)]
+
+        def send(u, carry):
+            px, pz, block = place(u)
+            pltpu.make_async_remote_copy(
+                src_ref=block, dst_ref=dst.at[row],
+                send_sem=zs_sem.at[8 + 4 * n + 2 * p + side], recv_sem=zr_sem.at[8 + 2 * n + p],
+                device_id={"gx": px, "gz": pz}, device_id_type=MESH,
+            ).start()
             return carry
 
-        lax.fori_loop(1, GROUP, send, 0)
-        pltpu.make_async_copy(
-            src.at[p, pl.ds(gz * BK, BK), pl.ds(gx * BI, BI)],
-            dst.at[p * GROUP + mine],
-            zr_sem.at[slot],
-        ).start()
+        lax.fori_loop(1, HALF, send, 0)
+        _, _, block = place(0)
+        pltpu.make_async_copy(block, dst.at[row], zr_sem.at[8 + 2 * n + p]).start()
 
     def wait_z(slot, ref):
         pltpu.make_async_copy(ref, ref, zr_sem.at[slot]).wait()
+
+    def wait_half(slot):
+        wait_z(slot, wide.at[0, pl.ds(0, N3 // 2)])
 
     def to_line(slot, src, dst, j0, rows):
         for d in range(1, GY):
@@ -152,9 +194,11 @@
     def wait_y(slot, ref):
         pltpu.make_async_copy(ref, ref, yr_sem.at[slot]).wait()
 
-    to_wide(0)
+    for side in range(SIDES):
+        to_near(0, side)
     to_line(0, ft, line_f, 0, BJ)
-    to_wide(1)
+    for side in range(SIDES):
+        to_near(1, side)
 
     for copy in loads:
         copy.wait()
@@ -163,7 +207,8 @@
 
     def split_a(n, carry):
         rows = pl.ds(pl.multiple_of(n * 128, 128), 128)
-        a_h[rows, :], a_l[rows, :] = split(a_f[rows, :])
+        part = pl.ds(pl.multiple_of((n % 2) * 128, 128), 128)
+        a_h[rows, :], a_l[rows, :] = split(s_two[n // 2, part, :])
         return carry
 
     lax.fori_loop(0, N1 // 128, split_a, 0)
@@ -211,21 +256,29 @@
     def add_w(rows, value):
         flat_w[rows, :] = flat_w[rows, :] + 2.0 * value
 
-    wait_z(0, wide.at[0])
-    along_wide(wide, s_one, 0)
-    to_home(1, s_one, one_home, 0)
+    for side in range(SIDES):
+        wait_half(side)
+        swap(0, side)
 
     wait_y(0, line_f)
     along_line(line_f, put_b)
     from_line(1, line_b, b_home)
-    along_wide(s_one, s_two, 0)
     along_line(line_b, put_w)
 
-    wait_z(1, wide.at[1])
-    along_wide(wide, s_one, 1)
-    to_home(1, s_one, one_home, 1)
-    to_home(2, s_two, two_home, 0)
-    along_wide(s_one, s_two, 1)
+    for side in range(SIDES):
+        wait_half(2 + side)
+        swap(1, side)
+
+    for p in range(PHASES):
+        for side in range(SIDES):
+            wait_half(4 + 2 * p + side)
+            along_wide(wide, s_one, 2 * p + side)
+            to_home(0, s_one, one_home, p, side)
+    for side in range(SIDES):
+        along_wide(s_one, s_two, side)
+        to_home(1, s_two, two_home, 0, side)
+    for side in range(SIDES):
+        along_wide(s_one, s_two, 2 + side)
 
     def squares(read):
         def add(n, carry):
@@ -238,11 +291,11 @@
     of_field = lax.fori_loop(0, BJ // 8, squares(lambda r: ft[r]), zero)
     wait_y(1, b_home)
 
-    wait_z(2, one_home.at[pl.ds(0, GROUP)])
+    wait_z(8, one_home.at[pl.ds(0, GROUP)])
     to_line(2, one_home, line_s, 0, GROUP)
     first = squares(lambda r: one_home[r] + b_home[r])
     of_first = lax.fori_loop(0, GROUP // 8, first, zero)
-    wait_z(3, one_home.at[pl.ds(GROUP, GROUP)])
+    wait_z(9, one_home.at[pl.ds(GROUP, GROUP)])
     to_line(3, one_home, line_s, GROUP, GROUP)
     of_first = lax.fori_loop(GROUP // 8, BJ // 8, first, of_first)
 
@@ -259,7 +312,8 @@
         pltpu.make_async_copy(norm_src, norm_y.at[pl.ds(gy, 1)], nr_sem.at[0]).start()
 
     send_norm_y()
-    to_home(2, s_two, two_home, 1)
+    for side in range(SIDES):
+        to_home(1, s_two, two_home, 1, side)
     pltpu.make_async_copy(norm_y, norm_y, nr_sem.at[0]).wait()
     norm_mid[0] = norm_y[0] + norm_y[1] + norm_y[2] + norm_y[3]
 
@@ -288,7 +342,7 @@
     step = (target_ratio * jnp.sqrt(ratio)).reshape(1, 1, BI)
     half = step * step / 2.0
 
-    wait_z(4, two_home.at[pl.ds(0, GROUP)])
+    wait_z(10, two_home.at[pl.ds(0, GROUP)])
     wait_y(4, w_home)
 
     def finish(n, carry):
@@ -297,11 +351,11 @@
         return carry
 
     lax.fori_loop(0, GROUP // 4, finish, 0)
-    wait_z(5, two_home.at[pl.ds(GROUP, GROUP)])
+    wait_z(11, two_home.at[pl.ds(GROUP, GROUP)])
     lax.fori_loop(GROUP // 4, BJ // 4, finish, 0)
 
-    for slot in range(6):
-        sent = ft.at[pl.ds(0, GROUP - 1)]
+    for slot in range(16):
+        sent = wide.at[0, pl.ds(0, N3 // 2)] if 4 <= slot < 8 else ft.at[pl.ds(0, HALF - 1)]
         pltpu.make_async_copy(sent, sent, zs_sem.at[slot]).wait()
     for slot, rows in ((0, 3 * BJ), (1, 3 * BJ), (2, 3 * GROUP), (3, 3 * GROUP), (4, 3 * BJ)):
         sent = line_f.at[pl.ds(0, rows)]
@@ -313,23 +367,22 @@
 
 
 def on_device(field, factor_a, factor_b, factor_c):
-    turned = jnp.transpose(field, (2, 0, 1))
     home = (BJ, BK, BI)
     vmem = pltpu.VMEM
     dma = pltpu.SemaphoreType.DMA
     scratch = [
-        vmem((N1, N1), F32), vmem((N2, N2), F32), vmem((N3, N3), F32),
+        vmem(home, F32), vmem((N2, N2), F32), vmem((N3, N3), F32),
         vmem((N1, N1), BF16), vmem((N1, N1), BF16),
         vmem((N2, N2), BF16), vmem((N2, N2), BF16),
         vmem((N3, N3), BF16), vmem((N3, N3), BF16),
-        vmem((PHASES, N3, N1), F32), vmem((PHASES, N3, N1), F32), vmem((PHASES, N3, N1), F32),
+        vmem((4, N3, N1), F32), vmem((4, N3, N1), F32), vmem((4, N3, N1), F32),
         vmem((N3, N1), BF16), vmem((N3, N1), BF16),
         vmem(home, F32), vmem(home, F32), vmem(home, F32), vmem(home, F32),
         vmem((N2, KY, BI), F32), vmem((N2, KY, BI), F32),
         vmem((N2, KY, BI), F32), vmem((N2, KY, BI), F32),
         vmem((1, 1, BI), F32), vmem((GY, 1, BI), F32),
         vmem((1, 1, BI), F32), vmem((GROUP, 1, BI), F32),
-        dma((3,)), dma((6,)), dma((6,)), dma((5,)), dma((5,)), dma((2,)), dma((2,)),
+        dma((6,)), dma((16,)), dma((12,)), dma((5,)), dma((5,)), dma((2,)), dma((2,)),
     ]
     result = pl.pallas_call(
         kernel,
@@ -341,7 +394,7 @@
             collective_id=0, has_side_effects=True, vmem_limit_bytes=60 * 1024 * 1024
         ),
         name="taylor",
-    )(turned, factor_a, factor_b, factor_c)
+    )(field, factor_a, factor_b, factor_c)
     return jnp.transpose(result, (1, 2, 0))
 
 

time: 162 us -> 159 us (0.981)
  local copies, waits for them, and re-layouts: 6 us -> 2.97 us
    unnamed x1 -> x0, local copies, waits for them, and re-layouts: 3.03 us -> none
where the time goes in v2:
time: 159 us; the launch traced here: 158 us
  Pallas kernels  155 us (97%)
  local copies, waits for them, and re-layouts  2.97 us (2%)
    pallas_call x1, Pallas kernels, on_device(): pl.pallas_call(kernel, out_shape=jax.ShapeDtypeStruct(home, F32), in_spec...  155 us

profile of v2, /device:TPU:1, one launch (start us, length us, event | category | flops | bytes accessed | tf_op | source)
XLA Modules:
  0.0 158.1 jit_solution(13659904910462736037)
XLA Ops:
  0.0 155.2 %taylor.1 = f32[128,32,128]{2,1,0:T(8,128)} custom-call(f32[32,128,128]{2,1,0:T(8,128)} %field.1, f32[1024,1024]{1,0:T(8,128)} %a_hbm.1, f32[512,512]{1,0:T(8,128)} %b_hbm.1, f32[256,256]{1,0:T(8,128)} %c_hbm.1), custom_call_target="tpu_custom_call" | custom-call | tf_op jit(solution)/shard_map/taylor/pallas_call | solution.py:387
  155.2 3.0 %copy.5 = f32[32,128,128]{2,1,0:T(8,128)} copy(f32[32,128,128]{1,0,2:T(8,128)} %bitcast.1) | data formatting | bytes 4194304 | tf_op jit(solution)/shard_map/transpose | solution.py:398

commit v3 on v2

--- a/solution.py
+++ b/solution.py
@@ -58,7 +58,7 @@
     wide, s_one, s_two, x_h, x_l,
     one_home, two_home, b_home, w_home,
     line_f, line_b, line_s, line_w,
-    norm_src, norm_y, norm_mid, norm_all,
+    l_h, l_l, norm_src, norm_y, norm_mid, norm_all,
     load_sem, zs_sem, zr_sem, ys_sem, yr_sem, ns_sem, nr_sem,
 ):
     gx, gy, gz = lax.axis_index("gx"), lax.axis_index("gy"), lax.axis_index("gz")
@@ -133,27 +133,30 @@
                 device_id={"gx": px, "gz": pz}, device_id_type=MESH,
             ).start()
 
-    def to_home(n, src, dst, p, side):
+    def to_home(n, src, dst, p, side, k0=0, depth=BK, late=0):
         sign = 1 - 2 * side
         ox, oz = device_at(z - side, x, c)
         row = p * GROUP + ox * GZ + oz
+        target = dst.at[row, pl.ds(k0, depth)]
+        arrived = zr_sem.at[8 + 2 * n + p + 3 * late]
 
         def place(u):
             px, pz = device_at(z - sign * (u // 8), x + u // 2, c + u)
-            return px, pz, src.at[2 * p + side, pl.ds(pz * BK, BK), pl.ds(px * BI, BI)]
+            block = src.at[2 * p + side, pl.ds(pz * BK + k0, depth), pl.ds(px * BI, BI)]
+            return px, pz, block
 
         def send(u, carry):
             px, pz, block = place(u)
             pltpu.make_async_remote_copy(
-                src_ref=block, dst_ref=dst.at[row],
-                send_sem=zs_sem.at[8 + 4 * n + 2 * p + side], recv_sem=zr_sem.at[8 + 2 * n + p],
+                src_ref=block, dst_ref=target,
+                send_sem=zs_sem.at[8 + 4 * n + 2 * p + side], recv_sem=arrived,
                 device_id={"gx": px, "gz": pz}, device_id_type=MESH,
             ).start()
             return carry
 
         lax.fori_loop(1, HALF, send, 0)
         _, _, block = place(0)
-        pltpu.make_async_copy(block, dst.at[row], zr_sem.at[8 + 2 * n + p]).start()
+        pltpu.make_async_copy(block, target, arrived).start()
 
     def wait_z(slot, ref):
         pltpu.make_async_copy(ref, ref, zr_sem.at[slot]).wait()
@@ -161,35 +164,35 @@
     def wait_half(slot):
         wait_z(slot, wide.at[0, pl.ds(0, N3 // 2)])
 
-    def to_line(slot, src, dst, j0, rows):
-        for d in range(1, GY):
-            py = (gy + d) % GY
+    def to_peer(slot, src, dst, j0, rows, py):
+        pltpu.make_async_remote_copy(
+            src_ref=src.at[pl.ds(j0, rows), pl.ds(py * KY, KY), :],
+            dst_ref=dst.at[pl.ds(gy * BJ + j0, rows)],
+            send_sem=ys_sem.at[slot], recv_sem=yr_sem.at[slot],
+            device_id={"gy": py}, device_id_type=MESH,
+        ).start()
+
+    def to_line(slot, src, dst, j0, rows, peers=(1, 2, 3), own=True):
+        for d in peers:
+            to_peer(slot, src, dst, j0, rows, (gy + d) % GY)
+        if own:
+            pltpu.make_async_copy(
+                src.at[pl.ds(j0, rows), pl.ds(gy * KY, KY), :],
+                dst.at[pl.ds(gy * BJ + j0, rows)],
+                yr_sem.at[slot],
+            ).start()
+
+    def from_line(slot, src, dst, d):
+        py = (gy + d) % GY
+        source, target = src.at[pl.ds(py * BJ, BJ)], dst.at[:, pl.ds(gy * KY, KY), :]
+        if d:
             pltpu.make_async_remote_copy(
-                src_ref=src.at[pl.ds(j0, rows), pl.ds(py * KY, KY), :],
-                dst_ref=dst.at[pl.ds(gy * BJ + j0, rows)],
+                src_ref=source, dst_ref=target,
                 send_sem=ys_sem.at[slot], recv_sem=yr_sem.at[slot],
                 device_id={"gy": py}, device_id_type=MESH,
             ).start()
-        pltpu.make_async_copy(
-            src.at[pl.ds(j0, rows), pl.ds(gy * KY, KY), :],
-            dst.at[pl.ds(gy * BJ + j0, rows)],
-            yr_sem.at[slot],
-        ).start()
-
-    def from_line(slot, src, dst):
-        for d in range(1, GY):
-            py = (gy + d) % GY
-            pltpu.make_async_remote_copy(
-                src_ref=src.at[pl.ds(py * BJ, BJ)],
-                dst_ref=dst.at[:, pl.ds(gy * KY, KY), :],
-                send_sem=ys_sem.at[slot], recv_sem=yr_sem.at[slot],
-                device_id={"gy": py}, device_id_type=MESH,
-            ).start()
-        pltpu.make_async_copy(
-            src.at[pl.ds(gy * BJ, BJ)],
-            dst.at[:, pl.ds(gy * KY, KY), :],
-            yr_sem.at[slot],
-        ).start()
+        else:
+            pltpu.make_async_copy(source, target, yr_sem.at[slot]).start()
 
     def wait_y(slot, ref):
         pltpu.make_async_copy(ref, ref, yr_sem.at[slot]).wait()
@@ -232,48 +235,63 @@
 
         lax.fori_loop(0, N1 // 256, tile, 0)
 
-    def along_line(src, put):
+    def cut_line(src, j0, rows):
         flat = src.reshape(N2 * KY, BI)
+        to = pl.ds(j0, rows)
+
+        def one(k, carry):
+            cols = pl.ds(pl.multiple_of(k * BI, BI), BI)
+            l_h[to, cols], l_l[to, cols] = split(flat[pl.ds(j0 * KY + k, rows, stride=KY), :])
+            return carry
+
+        lax.fori_loop(0, KY, one, 0)
+
+    def line_rows(d, dst, add):
+        j0 = pl.multiple_of((gy + d) % GY * BJ, BJ)
+        flat = dst.reshape(N2 * KY, BI)
+        b_hi, b_lo = b_h[pl.ds(j0, BJ), :], b_l[pl.ds(j0, BJ), :]
 
         def pair(q, carry):
-            cols = [flat[pl.ds(2 * q + e, N2, stride=KY), :] for e in range(2)]
-            xh, xl = split(jnp.concatenate(cols, axis=1))
-            total = dot(b_h[...], xh) + dot(b_l[...], xh) + dot(b_h[...], xl)
+            cols = pl.ds(pl.multiple_of(q * 2 * BI, 2 * BI), 2 * BI)
+            xh, xl = l_h[:, cols], l_l[:, cols]
+            total = dot(b_hi, xh) + dot(b_hi, xl) + dot(b_lo, xh)
             for e in range(2):
-                put(pl.ds(2 * q + e, N2, stride=KY), total[:, e * BI:(e + 1) * BI])
+                rows = pl.ds(j0 * KY + 2 * q + e, BJ, stride=KY)
+                part = total[:, e * BI:(e + 1) * BI]
+                flat[rows, :] = flat[rows, :] + 2.0 * part if add else part
             return carry
 
         lax.fori_loop(0, KY // 2, pair, 0)
-
-    flat_b, flat_w = line_b.reshape(N2 * KY, BI), line_w.reshape(N2 * KY, BI)
-
-    def put_b(rows, value):
-        flat_b[rows, :] = value
-
-    def put_w(rows, value):
-        flat_w[rows, :] = value
-
-    def add_w(rows, value):
-        flat_w[rows, :] = flat_w[rows, :] + 2.0 * value
 
     for side in range(SIDES):
         wait_half(side)
         swap(0, side)
 
     wait_y(0, line_f)
-    along_line(line_f, put_b)
-    from_line(1, line_b, b_home)
-    along_line(line_b, put_w)
+    cut_line(line_f, 0, N2)
+    for d in (1, 2, 3, 0):
+        line_rows(d, line_b, False)
+        from_line(1, line_b, b_home, d)
+    cut_line(line_b, 0, N2)
+    for d in range(GY):
+        line_rows(d, line_w, False)
 
     for side in range(SIDES):
         wait_half(2 + side)
         swap(1, side)
 
-    for p in range(PHASES):
-        for side in range(SIDES):
-            wait_half(4 + 2 * p + side)
-            along_wide(wide, s_one, 2 * p + side)
-            to_home(0, s_one, one_home, p, side)
+    k_early, k_late = (1 - gy // 2) * (BK // 2), (gy // 2) * (BK // 2)
+    for side in range(SIDES):
+        wait_half(4 + side)
+        along_wide(wide, s_one, side)
+        to_home(0, s_one, one_home, 0, side)
+    for side in range(SIDES):
+        wait_half(6 + side)
+        along_wide(wide, s_one, 2 + side)
+    for side in range(SIDES):
+        to_home(0, s_one, one_home, 1, side, k_early, BK // 2)
+    for side in range(SIDES):
+        to_home(0, s_one, one_home, 1, side, k_late, BK // 2, late=1)
     for side in range(SIDES):
         along_wide(s_one, s_two, side)
         to_home(1, s_two, two_home, 0, side)
@@ -295,8 +313,14 @@
     to_line(2, one_home, line_s, 0, GROUP)
     first = squares(lambda r: one_home[r] + b_home[r])
     of_first = lax.fori_loop(0, GROUP // 8, first, zero)
-    wait_z(9, one_home.at[pl.ds(GROUP, GROUP)])
-    to_line(3, one_home, line_s, GROUP, GROUP)
+    half_phase = one_home.at[pl.ds(0, GROUP), pl.ds(0, BK // 2)]
+    wait_z(9, half_phase)
+    for tile in range(2):
+        py = (1 - gy // 2) * 2 + tile
+        to_peer(3, one_home, line_s, GROUP, GROUP, py)
+    wait_z(12, half_phase)
+    to_peer(3, one_home, line_s, GROUP, GROUP, gy + 1 - 2 * (gy % 2))
+    to_line(3, one_home, line_s, GROUP, GROUP, peers=())
     of_first = lax.fori_loop(GROUP // 8, BJ // 8, first, of_first)
 
     lane = lax.broadcasted_iota(jnp.int32, (1, BI), 1)
@@ -330,9 +354,14 @@
     pltpu.make_async_copy(norm_mid, norm_all.at[pl.ds(mine, 1)], nr_sem.at[1]).start()
 
     wait_y(2, line_s.at[pl.ds(0, N2 // 2)])
+    for d in range(GY):
+        cut_line(line_s, d * BJ, GROUP)
     wait_y(3, line_s.at[pl.ds(0, N2 // 2)])
-    along_line(line_s, add_w)
-    from_line(4, line_w, w_home)
+    for d in range(GY):
+        cut_line(line_s, d * BJ + GROUP, GROUP)
+    for d in (2, 1, 3, 0):
+        line_rows(d, line_w, True)
+        from_line(4, line_w, w_home, d)
 
     pltpu.make_async_copy(norm_all, norm_all, nr_sem.at[1]).wait()
     sums = jnp.sum(norm_all[...], axis=0)
@@ -380,9 +409,10 @@
         vmem(home, F32), vmem(home, F32), vmem(home, F32), vmem(home, F32),
         vmem((N2, KY, BI), F32), vmem((N2, KY, BI), F32),
         vmem((N2, KY, BI), F32), vmem((N2, KY, BI), F32),
+        vmem((N2, KY * BI), BF16), vmem((N2, KY * BI), BF16),
         vmem((1, 1, BI), F32), vmem((GY, 1, BI), F32),
         vmem((1, 1, BI), F32), vmem((GROUP, 1, BI), F32),
-        dma((6,)), dma((16,)), dma((12,)), dma((5,)), dma((5,)), dma((2,)), dma((2,)),
+        dma((6,)), dma((16,)), dma((13,)), dma((5,)), dma((5,)), dma((2,)), dma((2,)),
     ]
     result = pl.pallas_call(
         kernel,

time: 159 us -> 159 us (level)
  no operation moved by 1% of the time
where the time goes in v3:
time: 159 us; the launch traced here: 158 us
  Pallas kernels  156 us (98%)
  local copies, waits for them, and re-layouts  2.97 us (2%)
    pallas_call x1, Pallas kernels, on_device(): pl.pallas_call(kernel, out_shape=jax.ShapeDtypeStruct(home, F32), in_spec...  156 us

profile of v3, /device:TPU:1, one launch (start us, length us, event | category | flops | bytes accessed | tf_op | source)
XLA Modules:
  0.0 158.5 jit_solution(6697094090046059084)
XLA Ops:
  0.0 155.5 %taylor.1 = f32[128,32,128]{2,1,0:T(8,128)} custom-call(f32[32,128,128]{2,1,0:T(8,128)} %field.1, f32[1024,1024]{1,0:T(8,128)} %a_hbm.1, f32[512,512]{1,0:T(8,128)} %b_hbm.1, f32[256,256]{1,0:T(8,128)} %c_hbm.1), custom_call_target="tpu_custom_call" | custom-call | tf_op jit(solution)/shard_map/taylor/pallas_call | solution.py:417
  155.5 3.0 %copy.5 = f32[32,128,128]{2,1,0:T(8,128)} copy(f32[32,128,128]{1,0,2:T(8,128)} %bitcast.1) | data formatting | bytes 4194304 | tf_op jit(solution)/shard_map/transpose | solution.py:428

commit v4 on v3

--- a/solution.py
+++ b/solution.py
@@ -18,6 +18,7 @@
 BK, BI, BJ = 32, 128, 128
 N1, N2, N3 = 1024, 512, 256
 KY = BK // GY
+PITCH = BK + 8
 PHASES = 2
 SIDES = 2
 HALF = GROUP // SIDES
@@ -34,17 +35,6 @@
 
 def dot_t(a, b):
     return lax.dot_general(a, b, (((1,), (1,)), ((), ())), preferred_element_type=F32)
-
-
-def member(t, gx, gz):
-    z, x, c = (gx // 2) * 2 + gz // 4, gz % 4, gx % 2
-    m, rest = t // 8, t % 8
-    odd = m % 2
-    dz = odd * ((m + 1) // 2) + (1 - odd) * (8 - m // 2)
-    z2 = (z + dz) % 8
-    x2 = (x + rest // 2) % 4
-    c2 = (c + rest) % 2
-    return (z2 // 2) * 2 + c2, (z2 % 2) * 4 + x2
 
 
 def device_at(z, x, c):
@@ -64,6 +54,22 @@
     gx, gy, gz = lax.axis_index("gx"), lax.axis_index("gy"), lax.axis_index("gz")
     mine = gx * GZ + gz
     z, x, c = (gx // 2) * 2 + gz // 4, gz % 4, gx % 2
+    columns = [((x + s // 2) % 4, (c + s) % 2) for s in range(8)]
+
+    def at(z2, s):
+        return (z2 // 2) * 2 + columns[s][1], (z2 % 2) * 4 + columns[s][0]
+
+    def all_others(visit):
+        def ring(n, carry):
+            odd = n % 2
+            z2 = (z + 4 + odd * ((n + 1) // 2) - (1 - odd) * (n // 2)) % 8
+            for s in range(8):
+                visit(*at(z2, s))
+            return carry
+
+        lax.fori_loop(0, 7, ring, 0)
+        for s in range(1, 8):
+            visit(*at(z, s))
 
     pieces = [(c_hbm, c_f), (b_hbm, b_f)]
     pieces += [(a_hbm.at[pl.ds(n * N3, N3)], s_two.at[n]) for n in range(N1 // N3)]
@@ -75,48 +81,54 @@
 
     barrier = pltpu.get_barrier_semaphore()
 
-    def greet(t, carry):
-        px, pz = member(t, gx, gz)
+    def greet(px, pz):
         pl.semaphore_signal(barrier, inc=1, device_id={"gx": px, "gz": pz}, device_id_type=MESH)
-        return carry
-
-    lax.fori_loop(1, GROUP, greet, 0)
+
     for d in range(1, GY):
         pl.semaphore_signal(
             barrier, inc=1, device_id={"gy": (gy + d) % GY}, device_id_type=MESH
         )
-
-    flat_ft = ft.reshape(BJ * BK, BI)
+    all_others(greet)
+
+    flat_ft = ft.reshape(BJ * PITCH, BI)
 
     def turn(k, carry):
-        flat_ft[pl.ds(k, BJ, stride=BK), :] = field[k].T
+        flat_ft[pl.ds(k, BJ, stride=PITCH), :] = field[k].T
         return carry
 
     lax.fori_loop(0, BK, turn, 0)
     pl.semaphore_wait(barrier, GROUP - 1 + GY - 1)
 
+    def half_ring(sign, send):
+        def ring(n, carry):
+            for s in range(8):
+                send((z + sign * n) % 8, s)
+            return carry
+
+        lax.fori_loop(1, 4, ring, 0)
+        for s in range(1, 8):
+            send(z, s)
+
     def to_near(p, side):
         sign = 1 - 2 * side
 
-        def place(u):
-            up = sign * (u // 8)
-            px, pz = device_at(z + up, x + u // 2, c + u)
-            ox, oz = device_at(z + up - side, x + u // 2, c + u)
-            src = ft.at[p * GROUP + ox * GZ + oz]
+        def place(z2, s):
+            px, pz = at(z2, s)
+            ox, oz = at((z2 - side) % 8, s)
+            src = ft.at[p * GROUP + ox * GZ + oz, pl.ds(0, BK)]
             dst = wide.at[2 * p + side, pl.ds(gz * BK, BK), pl.ds(gx * BI, BI)]
             return px, pz, src, dst
 
-        def send(u, carry):
-            px, pz, src, dst = place(u)
+        def send(z2, s):
+            px, pz, src, dst = place(z2, s)
             pltpu.make_async_remote_copy(
                 src_ref=src, dst_ref=dst,
                 send_sem=zs_sem.at[2 * p + side], recv_sem=zr_sem.at[2 * p + side],
                 device_id={"gx": px, "gz": pz}, device_id_type=MESH,
             ).start()
-            return carry
-
-        lax.fori_loop(1, HALF, send, 0)
-        _, _, src, dst = place(0)
+
+        half_ring(sign, send)
+        _, _, src, dst = place(z, 0)
         pltpu.make_async_copy(src, dst, zr_sem.at[2 * p + side]).start()
 
     def swap(p, side):
@@ -140,22 +152,21 @@
         target = dst.at[row, pl.ds(k0, depth)]
         arrived = zr_sem.at[8 + 2 * n + p + 3 * late]
 
-        def place(u):
-            px, pz = device_at(z - sign * (u // 8), x + u // 2, c + u)
+        def place(z2, s):
+            px, pz = at(z2, s)
             block = src.at[2 * p + side, pl.ds(pz * BK + k0, depth), pl.ds(px * BI, BI)]
             return px, pz, block
 
-        def send(u, carry):
-            px, pz, block = place(u)
+        def send(z2, s):
+            px, pz, block = place(z2, s)
             pltpu.make_async_remote_copy(
                 src_ref=block, dst_ref=target,
                 send_sem=zs_sem.at[8 + 4 * n + 2 * p + side], recv_sem=arrived,
                 device_id={"gx": px, "gz": pz}, device_id_type=MESH,
             ).start()
-            return carry
-
-        lax.fori_loop(1, HALF, send, 0)
-        _, _, block = place(0)
+
+        half_ring(-sign, send)
+        _, _, block = place(z, 0)
         pltpu.make_async_copy(block, target, arrived).start()
 
     def wait_z(slot, ref):
@@ -272,14 +283,15 @@
     for d in (1, 2, 3, 0):
         line_rows(d, line_b, False)
         from_line(1, line_b, b_home, d)
+
+    for side in range(SIDES):
+        wait_half(2 + side)
+        swap(1, side)
+
     cut_line(line_b, 0, N2)
     for d in range(GY):
         line_rows(d, line_w, False)
 
-    for side in range(SIDES):
-        wait_half(2 + side)
-        swap(1, side)
-
     k_early, k_late = (1 - gy // 2) * (BK // 2), (gy // 2) * (BK // 2)
     for side in range(SIDES):
         wait_half(4 + side)
@@ -295,6 +307,10 @@
     for side in range(SIDES):
         along_wide(s_one, s_two, side)
         to_home(1, s_two, two_home, 0, side)
+
+    wait_z(8, one_home.at[pl.ds(0, GROUP)])
+    to_line(2, one_home, line_s, 0, GROUP)
+
     for side in range(SIDES):
         along_wide(s_one, s_two, 2 + side)
 
@@ -306,13 +322,11 @@
         return add
 
     zero = jnp.zeros((1, BI), F32)
-    of_field = lax.fori_loop(0, BJ // 8, squares(lambda r: ft[r]), zero)
+    of_field = lax.fori_loop(0, BJ // 8, squares(lambda r: ft[r, pl.ds(0, BK)]), zero)
     wait_y(1, b_home)
-
-    wait_z(8, one_home.at[pl.ds(0, GROUP)])
-    to_line(2, one_home, line_s, 0, GROUP)
     first = squares(lambda r: one_home[r] + b_home[r])
     of_first = lax.fori_loop(0, GROUP // 8, first, zero)
+
     half_phase = one_home.at[pl.ds(0, GROUP), pl.ds(0, BK // 2)]
     wait_z(9, half_phase)
     for tile in range(2):
@@ -338,21 +352,6 @@
     send_norm_y()
     for side in range(SIDES):
         to_home(1, s_two, two_home, 1, side)
-    pltpu.make_async_copy(norm_y, norm_y, nr_sem.at[0]).wait()
-    norm_mid[0] = norm_y[0] + norm_y[1] + norm_y[2] + norm_y[3]
-
-    def send_norm(t, carry):
-        px, pz = member(t, gx, gz)
-        pltpu.make_async_remote_copy(
-            src_ref=norm_mid, dst_ref=norm_all.at[pl.ds(mine, 1)],
-            send_sem=ns_sem.at[1], recv_sem=nr_sem.at[1],
-            device_id={"gx": px, "gz": pz}, device_id_type=MESH,
-        ).start()
-        return carry
-
-    lax.fori_loop(1, GROUP, send_norm, 0)
-    pltpu.make_async_copy(norm_mid, norm_all.at[pl.ds(mine, 1)], nr_sem.at[1]).start()
-
     wait_y(2, line_s.at[pl.ds(0, N2 // 2)])
     for d in range(GY):
         cut_line(line_s, d * BJ, GROUP)
@@ -363,6 +362,19 @@
         line_rows(d, line_w, True)
         from_line(4, line_w, w_home, d)
 
+    pltpu.make_async_copy(norm_y, norm_y, nr_sem.at[0]).wait()
+    norm_mid[0] = norm_y[0] + norm_y[1] + norm_y[2] + norm_y[3]
+
+    def send_norm(px, pz):
+        pltpu.make_async_remote_copy(
+            src_ref=norm_mid, dst_ref=norm_all.at[pl.ds(mine, 1)],
+            send_sem=ns_sem.at[1], recv_sem=nr_sem.at[1],
+            device_id={"gx": px, "gz": pz}, device_id_type=MESH,
+        ).start()
+
+    all_others(send_norm)
+    pltpu.make_async_copy(norm_mid, norm_all.at[pl.ds(mine, 1)], nr_sem.at[1]).start()
+
     pltpu.make_async_copy(norm_all, norm_all, nr_sem.at[1]).wait()
     sums = jnp.sum(norm_all[...], axis=0)
     size_field = jnp.sum(jnp.where(lane == 0, sums, 0.0))
@@ -376,7 +388,7 @@
 
     def finish(n, carry):
         r = pl.ds(n * 4, 4)
-        out[r] = (ft[r] - step * (one_home[r] + b_home[r])) + half * (two_home[r] + w_home[r])
+        out[r] = (ft[r, pl.ds(0, BK)] - step * (one_home[r] + b_home[r])) + half * (two_home[r] + w_home[r])
         return carry
 
     lax.fori_loop(0, GROUP // 4, finish, 0)
@@ -384,7 +396,7 @@
     lax.fori_loop(GROUP // 4, BJ // 4, finish, 0)
 
     for slot in range(16):
-        sent = wide.at[0, pl.ds(0, N3 // 2)] if 4 <= slot < 8 else ft.at[pl.ds(0, HALF - 1)]
+        sent = wide.at[0, pl.ds(0, N3 // 2)] if 4 <= slot < 8 else one_home.at[pl.ds(0, HALF - 1)]
         pltpu.make_async_copy(sent, sent, zs_sem.at[slot]).wait()
     for slot, rows in ((0, 3 * BJ), (1, 3 * BJ), (2, 3 * GROUP), (3, 3 * GROUP), (4, 3 * BJ)):
         sent = line_f.at[pl.ds(0, rows)]
@@ -400,7 +412,7 @@
     vmem = pltpu.VMEM
     dma = pltpu.SemaphoreType.DMA
     scratch = [
-        vmem(home, F32), vmem((N2, N2), F32), vmem((N3, N3), F32),
+        vmem((BJ, PITCH, BI), F32), vmem((N2, N2), F32), vmem((N3, N3), F32),
         vmem((N1, N1), BF16), vmem((N1, N1), BF16),
         vmem((N2, N2), BF16), vmem((N2, N2), BF16),
         vmem((N3, N3), BF16), vmem((N3, N3), BF16),

time: 159 us -> 147 us (0.925)
  Pallas kernels: 156 us -> 144 us
    pallas_call x1, Pallas kernels: 156 us -> 144 us  [on_device(): pl.pallas_call(kernel, out_shape=jax.ShapeDtypeStruct(home, F32), in_spec...]
where the time goes in v4:
time: 147 us
  Pallas kernels  144 us (98%)
  local copies, waits for them, and re-layouts  2.97 us (2%)
    pallas_call x1, Pallas kernels, on_device(): pl.pallas_call(kernel, out_shape=jax.ShapeDtypeStruct(home, F32), in_spec...  144 us
    transpose x1, local copies, waits for them, and re-layouts, on_device(): return jnp.transpose(result, (1, 2, 0))  2.97 us

profile of v4, /device:TPU:1, one launch (start us, length us, event | category | flops | bytes accessed | tf_op | source)
XLA Modules:
  0.0 147.1 jit_solution(8110843014397885564)
XLA Ops:
  0.0 144.1 %taylor.1 = f32[128,32,128]{2,1,0:T(8,128)} custom-call(f32[32,128,128]{2,1,0:T(8,128)} %field.1, f32[1024,1024]{1,0:T(8,128)} %a_hbm.1, f32[512,512]{1,0:T(8,128)} %b_hbm.1, f32[256,256]{1,0:T(8,128)} %c_hbm.1), custom_call_target="tpu_custom_call" | custom-call | tf_op jit(solution)/shard_map/taylor/pallas_call | solution.py:429
  144.1 3.0 %copy.5 = f32[32,128,128]{2,1,0:T(8,128)} copy(f32[32,128,128]{1,0,2:T(8,128)} %bitcast.1) | data formatting | bytes 4194304 | tf_op jit(solution)/shard_map/transpose | solution.py:440

commit v5 on v4

--- a/solution.py
+++ b/solution.py
@@ -43,8 +43,8 @@
 
 
 def kernel(
-    field, a_hbm, b_hbm, c_hbm, out,
-    ft, b_f, c_f, a_h, a_l, b_h, b_l, c_h, c_l,
+    field_hbm, a_hbm, b_hbm, c_hbm, out,
+    field, ft, b_f, c_f, a_h, a_l, b_h, b_l, c_h, c_l,
     wide, s_one, s_two, x_h, x_l,
     one_home, two_home, b_home, w_home,
     line_f, line_b, line_s, line_w,
@@ -76,8 +76,8 @@
     loads = [
         pltpu.make_async_copy(src, dst, load_sem.at[n]) for n, (src, dst) in enumerate(pieces)
     ]
-    for copy in loads:
-        copy.start()
+    field_load = pltpu.make_async_copy(field_hbm, field, load_sem.at[6])
+    field_load.start()
 
     barrier = pltpu.get_barrier_semaphore()
 
@@ -96,13 +96,16 @@
         flat_ft[pl.ds(k, BJ, stride=PITCH), :] = field[k].T
         return carry
 
+    field_load.wait()
+    for copy in loads:
+        copy.start()
     lax.fori_loop(0, BK, turn, 0)
     pl.semaphore_wait(barrier, GROUP - 1 + GY - 1)
 
     def half_ring(sign, send):
         def ring(n, carry):
             for s in range(8):
-                send((z + sign * n) % 8, s)
+                send((z + sign * (4 - n)) % 8, s)
             return carry
 
         lax.fori_loop(1, 4, ring, 0)
@@ -150,7 +153,7 @@
         ox, oz = device_at(z - side, x, c)
         row = p * GROUP + ox * GZ + oz
         target = dst.at[row, pl.ds(k0, depth)]
-        arrived = zr_sem.at[8 + 2 * n + p + 3 * late]
+        arrived = zr_sem.at[13 + late - 2 * p if late else 8 + 2 * n + p]
 
         def place(z2, s):
             px, pz = at(z2, s)
@@ -292,24 +295,30 @@
     for d in range(GY):
         line_rows(d, line_w, False)
 
-    k_early, k_late = (1 - gy // 2) * (BK // 2), (gy // 2) * (BK // 2)
-    for side in range(SIDES):
-        wait_half(4 + side)
-        along_wide(wide, s_one, side)
-        to_home(0, s_one, one_home, 0, side)
-    for side in range(SIDES):
-        wait_half(6 + side)
-        along_wide(wide, s_one, 2 + side)
-    for side in range(SIDES):
-        to_home(0, s_one, one_home, 1, side, k_early, BK // 2)
-    for side in range(SIDES):
-        to_home(0, s_one, one_home, 1, side, k_late, BK // 2, late=1)
+    mate = gy + 1 - 2 * (gy % 2)
+    k_early = (1 - gy // 2) * (BK // 2)
+    parts = ((k_early, BK // 2, 0), (mate * KY, KY, 1), (gy * KY, KY, 2))
+    for p in range(PHASES):
+        for side in range(SIDES):
+            wait_half(4 + 2 * p + side)
+            along_wide(wide, s_one, 2 * p + side)
+        for k0, depth, late in parts:
+            for side in range(SIDES):
+                to_home(0, s_one, one_home, p, side, k0, depth, late)
     for side in range(SIDES):
         along_wide(s_one, s_two, side)
         to_home(1, s_two, two_home, 0, side)
 
-    wait_z(8, one_home.at[pl.ds(0, GROUP)])
-    to_line(2, one_home, line_s, 0, GROUP)
+    def forward(p):
+        wait_z(8 + p, one_home.at[pl.ds(0, GROUP), pl.ds(0, BK // 2)])
+        for tile in range(2):
+            to_peer(2 + p, one_home, line_s, p * GROUP, GROUP, (1 - gy // 2) * 2 + tile)
+        wait_z(14 - 2 * p, one_home.at[pl.ds(0, GROUP), pl.ds(0, KY)])
+        to_peer(2 + p, one_home, line_s, p * GROUP, GROUP, mate)
+        wait_z(15 - 2 * p, one_home.at[pl.ds(0, GROUP), pl.ds(0, KY)])
+        to_line(2 + p, one_home, line_s, p * GROUP, GROUP, peers=())
+
+    forward(0)
 
     for side in range(SIDES):
         along_wide(s_one, s_two, 2 + side)
@@ -327,14 +336,7 @@
     first = squares(lambda r: one_home[r] + b_home[r])
     of_first = lax.fori_loop(0, GROUP // 8, first, zero)
 
-    half_phase = one_home.at[pl.ds(0, GROUP), pl.ds(0, BK // 2)]
-    wait_z(9, half_phase)
-    for tile in range(2):
-        py = (1 - gy // 2) * 2 + tile
-        to_peer(3, one_home, line_s, GROUP, GROUP, py)
-    wait_z(12, half_phase)
-    to_peer(3, one_home, line_s, GROUP, GROUP, gy + 1 - 2 * (gy % 2))
-    to_line(3, one_home, line_s, GROUP, GROUP, peers=())
+    forward(1)
     of_first = lax.fori_loop(GROUP // 8, BJ // 8, first, of_first)
 
     lane = lax.broadcasted_iota(jnp.int32, (1, BI), 1)
@@ -350,17 +352,14 @@
         pltpu.make_async_copy(norm_src, norm_y.at[pl.ds(gy, 1)], nr_sem.at[0]).start()
 
     send_norm_y()
-    for side in range(SIDES):
-        to_home(1, s_two, two_home, 1, side)
     wait_y(2, line_s.at[pl.ds(0, N2 // 2)])
     for d in range(GY):
         cut_line(line_s, d * BJ, GROUP)
     wait_y(3, line_s.at[pl.ds(0, N2 // 2)])
     for d in range(GY):
         cut_line(line_s, d * BJ + GROUP, GROUP)
-    for d in (2, 1, 3, 0):
-        line_rows(d, line_w, True)
-        from_line(4, line_w, w_home, d)
+    line_rows(2, line_w, True)
+    from_line(4, line_w, w_home, 2)
 
     pltpu.make_async_copy(norm_y, norm_y, nr_sem.at[0]).wait()
     norm_mid[0] = norm_y[0] + norm_y[1] + norm_y[2] + norm_y[3]
@@ -374,6 +373,12 @@
 
     all_others(send_norm)
     pltpu.make_async_copy(norm_mid, norm_all.at[pl.ds(mine, 1)], nr_sem.at[1]).start()
+    for side in range(SIDES):
+        to_home(1, s_two, two_home, 1, side)
+
+    for d in (1, 3, 0):
+        line_rows(d, line_w, True)
+        from_line(4, line_w, w_home, d)
 
     pltpu.make_async_copy(norm_all, norm_all, nr_sem.at[1]).wait()
     sums = jnp.sum(norm_all[...], axis=0)
@@ -412,7 +417,7 @@
     vmem = pltpu.VMEM
     dma = pltpu.SemaphoreType.DMA
     scratch = [
-        vmem((BJ, PITCH, BI), F32), vmem((N2, N2), F32), vmem((N3, N3), F32),
+        vmem((BK, BI, BJ), F32), vmem((BJ, PITCH, BI), F32), vmem((N2, N2), F32), vmem((N3, N3), F32),
         vmem((N1, N1), BF16), vmem((N1, N1), BF16),
         vmem((N2, N2), BF16), vmem((N2, N2), BF16),
         vmem((N3, N3), BF16), vmem((N3, N3), BF16),
@@ -424,12 +429,12 @@
         vmem((N2, KY * BI), BF16), vmem((N2, KY * BI), BF16),
         vmem((1, 1, BI), F32), vmem((GY, 1, BI), F32),
         vmem((1, 1, BI), F32), vmem((GROUP, 1, BI), F32),
-        dma((6,)), dma((16,)), dma((13,)), dma((5,)), dma((5,)), dma((2,)), dma((2,)),
+        dma((7,)), dma((16,)), dma((16,)), dma((5,)), dma((5,)), dma((2,)), dma((2,)),
     ]
     result = pl.pallas_call(
         kernel,
         out_shape=jax.ShapeDtypeStruct(home, F32),
-        in_specs=[pl.BlockSpec(memory_space=pltpu.VMEM)] + [pl.BlockSpec(memory_space=pl.ANY)] * 3,
+        in_specs=[pl.BlockSpec(memory_space=pl.ANY)] * 4,
         out_specs=pl.BlockSpec(memory_space=pltpu.VMEM),
         scratch_shapes=scratch,
         compiler_params=pltpu.CompilerParams(

time: 147 us -> 144 us (0.980)
  Pallas kernels: 144 us -> 141 us
    pallas_call x1, Pallas kernels: 144 us -> 141 us  [on_device(): pl.pallas_call(kernel, out_shape=jax.ShapeDtypeStruct(home, F32), in_spec...]
where the time goes in v5:
time: 144 us
  Pallas kernels  141 us (98%)
  local copies, waits for them, and re-layouts  2.97 us (2%)
    pallas_call x1, Pallas kernels, on_device(): pl.pallas_call(kernel, out_shape=jax.ShapeDtypeStruct(home, F32), in_spec...  141 us
    transpose x1, local copies, waits for them, and re-layouts, on_device(): return jnp.transpose(result, (1, 2, 0))  2.97 us

profile of v5, /device:TPU:1, one launch (start us, length us, event | category | flops | bytes accessed | tf_op | source)
XLA Modules:
  0.0 143.8 jit_solution(15244522761502418511)
XLA Ops:
  0.0 140.8 %taylor.1 = f32[128,32,128]{2,1,0:T(8,128)} custom-call(f32[32,128,128]{2,1,0:T(8,128)} %field_hbm.1, f32[1024,1024]{1,0:T(8,128)} %a_hbm.1, f32[512,512]{1,0:T(8,128)} %b_hbm.1, f32[256,256]{1,0:T(8,128)} %c_hbm.1), custom_call_target="tpu_custom_call" | custom-call | tf_op jit(solution)/shard_map/taylor/pallas_call | solution.py:434
  140.9 3.0 %copy.5 = f32[32,128,128]{2,1,0:T(8,128)} copy(f32[32,128,128]{1,0,2:T(8,128)} %bitcast.1) | data formatting | bytes 4194304 | tf_op jit(solution)/shard_map/transpose | solution.py:445
